TPU v7x, 32 devices: a whole 2x2x4 slice. The times are simulated.
32 devices in a mesh: row: 4 (over y, x), col: 8 (over z, core).
Axes of the slice: x: 2, y: 2, z: 4, core: 2. Of those that a mesh axis runs over, the one named last changes fastest.
Arguments:
- psi: bfloat16 [8192, 8192], P(('row', 'col')), may hold values from -0.125 to 0.125
- hpsi: bfloat16 [8192, 128], P(('row', 'col')), may hold values from -0.796875 to 0.796875
- slab_counts: int32 [32], P(('row', 'col')), may hold values from 1 to 256, 6144 in all
- matrix: float32 [4, 2048, 8, 1024], P('row', None, 'col'), as said below
Outputs:
- reduced: float32 [4, 2048, 8, 1024], P('row', None, 'col')
Inputs may be any that keep to these rules, and one draw needn't show every extreme that they name: Slab k's live plane waves are its first slab_counts[k] slots; the rest are padding; the counts sum to 3 * 256 * 32 // 4. The stored matrix is symmetric.
All inputs are finite; a program needn't handle non-finite values.
Results may differ from a plain program's by a relative error of at most 0.0003.
Values sent between devices are 32-bit elements; how exact they have to be, the bound alone decides.
No kernel may reach another device: no remote copies, remote signals or barrier semaphores. Data moves between devices by JAX's collectives and lax.ppermute only.
A program may use at most 64 MiB of HBM per device.

v0:
```python
import jax
import jax.numpy as jnp
from jax import lax
from jax.sharding import PartitionSpec as P

TILE = 16
HIGH = lax.Precision.HIGHEST


def lower_solve(factor, rhs):
    return lax.linalg.triangular_solve(factor, rhs, left_side=True, lower=True)


def invert_shifted(shifted):
    normal = jnp.dot(shifted.T, shifted, precision=HIGH)
    factor = jnp.linalg.cholesky(normal)
    first = lower_solve(factor, shifted.T)
    return lax.linalg.triangular_solve(factor, first, left_side=True, lower=True, transpose_a=True)


def per_device(psi, hpsi, slab_counts, matrix):
    prow_id = lax.axis_index("row")
    pcol_id = lax.axis_index("col")
    n_row = lax.axis_size("row")
    n_col = lax.axis_size("col")
    slots = psi.shape[0]
    panel = hpsi.shape[1]
    local_rows = matrix.shape[1]
    local_cols = matrix.shape[3]
    tiles_r = local_rows // TILE
    tiles_c = local_cols // TILE
    valid = jnp.arange(slots, dtype=jnp.int32) < slab_counts[0]
    hcols = jnp.where(valid[:, None], hpsi, jnp.zeros_like(hpsi))
    local_r = jnp.arange(local_rows, dtype=jnp.int32)
    local_c = jnp.arange(local_cols, dtype=jnp.int32)
    row_global = (local_r // TILE * n_row + prow_id) * TILE + local_r % TILE
    col_global = (local_c // TILE * n_col + pcol_id) * TILE + local_c % TILE
    partial_value = lax.dot_general(
        psi, hcols, (((0,), (0,)), ((), ())), preferred_element_type=jnp.float32
    )
    whole = lax.psum(partial_value, ("row", "col"))
    prow = lax.dynamic_index_in_dim(
        whole.reshape(tiles_r, n_row, TILE, panel), prow_id, 1, keepdims=False
    ).reshape(local_rows, panel)
    scols = lax.dynamic_index_in_dim(
        whole.reshape(tiles_c, n_col, TILE, panel), pcol_id, 1, keepdims=False
    ).reshape(local_cols, panel)
    span = jnp.arange(panel, dtype=jnp.int32)
    lower_r = jnp.where((row_global >= panel)[:, None], prow, jnp.zeros_like(prow))
    lower_c = jnp.where((col_global >= panel)[:, None], scols, jnp.zeros_like(scols))
    top_select = (row_global[None, :] == panel + span[:, None]).astype(jnp.float32)
    gram_part = jnp.dot(lower_r.T, lower_r, precision=HIGH)
    top_part = jnp.dot(top_select, prow, precision=HIGH)
    gram, top_rows = lax.psum((gram_part, top_part), "row")
    factor = jnp.linalg.cholesky(gram)
    basis_r = lower_solve(factor, lower_r.T).T
    basis_c = lower_solve(factor, lower_c.T).T
    top = lower_solve(factor, top_rows.T).T
    inverse = invert_shifted(jnp.eye(panel, dtype=jnp.float32) - top)
    embed_r = (row_global[:, None] == panel + span[None, :]).astype(jnp.float32)
    embed_c = (col_global[:, None] == panel + span[None, :]).astype(jnp.float32)
    reflect_r = basis_r - embed_r
    reflect_c = basis_c - embed_c
    stored = matrix[0, :, 0, :]
    col_select = (col_global[None, :] == span[:, None]).astype(jnp.float32)
    row_select = (row_global[None, :] == span[:, None]).astype(jnp.float32)
    left = jnp.dot(prow, col_select, precision=HIGH)
    upper = lax.dot_general(row_select, scols, (((0,), (1,)), ((), ())), precision=HIGH)
    inside_r = (row_global < panel)[:, None]
    inside_c = (col_global < panel)[None, :]
    refreshed = jnp.where(
        inside_r & inside_c,
        0.5 * (left + upper),
        jnp.where(inside_c, left, jnp.where(inside_r, upper, stored)),
    )
    zpart = jnp.dot(refreshed, reflect_c, precision=HIGH)
    zrows = lax.psum(zpart, "col")
    upart = lax.dot_general(refreshed, reflect_r, (((0,), (0,)), ((), ())), precision=HIGH)
    ucols = lax.psum(upart, "row")
    wmat = lax.psum(jnp.dot(reflect_r.T, zrows, precision=HIGH), "row")
    core = jnp.dot(jnp.dot(inverse, wmat, precision=HIGH), inverse.T, precision=HIGH)
    first = jnp.dot(reflect_r, jnp.dot(inverse, ucols.T, precision=HIGH), precision=HIGH)
    second = jnp.dot(
        jnp.dot(zrows, inverse.T, precision=HIGH) - jnp.dot(reflect_r, core, precision=HIGH),
        reflect_c.T,
        precision=HIGH,
    )
    return (refreshed - first - second)[None, :, None, :]


def solution(mesh):
    in_specs = (
        P(("row", "col"), None),
        P(("row", "col"), None),
        P(("row", "col")),
        P("row", None, "col", None),
    )
    out_specs = P("row", None, "col", None)
    return jax.shard_map(
        per_device, mesh=mesh, in_specs=in_specs, out_specs=out_specs, check_vma=False
    )
```

profile of v0, /device:TPU:0, one launch (start us, length us, event | category | flops | bytes accessed | tf_op | source)
XLA Modules:
  0.0 421.6 jit_solution(14257435263756658271)
XLA Ops:
  6.5 0.0 all-reduce.6.cloned.1.call-start
  7.2 5.1 %convolution_bitcast_fusion = f32[8192,128]{0,1:T(8,128)} fusion(bf16[256,8192]{1,0:T(8,128)(2,1)} %param.7, bf16[256,128]{1,0:T(8,128)(2,1)} %param.8, pred[256]{0:T(512)(128)(4,1)S(1)} %iota_compare_fusion.9), kind=kOutput, calls=%fused_computation | convolution fusion | flops 536903680 | bytes 8454400 | tf_op jit(solution)/shard_map/dot_general | solution.py:38
  12.3 0.0 all-reduce.6.cloned.1.call-update
  12.3 0.0 all-reduce.8.cloned.1.call-start
  12.5 0.1 fusion.18
  12.6 145.3 %all-reduce.6.cloned.1.call-done = f32[8192,128]{0,1:T(8,128)} async-done(((f32[8192,128]{0,1:T(8,128)}), f32[8192,128]{0,1:T(8,128)}) %all-reduce.6.cloned.1.call-update) | async-done | bytes 4194320 | tf_op jit(solution)/shard_map/psum | solution.py:41
  157.9 5.6 %copy.11 = f32[8192,128]{1,0:T(8,128)} copy(f32[8192,128]{0,1:T(8,128)} %all-reduce.6.cloned.1.call-done) | data formatting | bytes 8388608 | tf_op jit(solution)/shard_map/psum | solution.py:41
  163.4 1.6 broadcast_select_fusion
  165.0 2.4 convolution_bitcast_fusion.1
  167.5 0.0 all-reduce.8.cloned.1.call-update
  167.5 0.0 all-reduce.10.cloned.1.call-start
  167.5 3.6 fusion.10
  171.1 1.3 broadcast_select_fusion.1
  172.4 11.0 %fusion.1 = f32[2048,1024]{1,0:T(8,128)} fusion(f32[2048,1024]{1,0:T(8,128)S(1)} %fusion.10, f32[1,2048,1,1024]{3,2,1,0:T(1,128)} %param.10, pred[1024]{0:T(1024)(128)(4,1)S(1)} %broadcast_compare_fusion.1, pred[2048]{0:T(1024)(128)(4,1)S(1)} %broadcast_compare_fusion, f32[1024,128]{1,0:T(8,128)S(1)} %bitcast.89, s32[2048]{0:T(1024)S(1)} %fusion.60), kind=kOutput, calls=%fused_computation.3 | convolution fusion | flops 3234332672 | bytes 25701376 | tf_op jit(solution)/shard_map/dot_general | solution.py:68
  183.3 1.6 fusion.4
  185.0 23.8 %all-reduce.8.cloned.1.call-done = f32[128,128]{0,1:T(8,128)} async-done(((f32[128,128]{0,1:T(8,128)}), f32[128,128]{0,1:T(8,128)}) %all-reduce.8.cloned.1.call-update) | async-done | bytes 65552 | tf_op jit(solution)/shard_map/psum | solution.py:54
  208.8 0.9 copy.16
  209.7 0.9 fusion.29
  210.5 11.7 %cholesky.44 = f32[128,128]{1,0:T(8,128)S(1)} custom-call(f32[128,128]{1,0:T(8,128)S(1)} %fusion.29), custom_call_target="Cholesky" | custom-call | tf_op jit(solution)/shard_map/jit(cholesky)/cholesky | solution.py:55
  222.3 0.7 compare_reduce_fusion.1
  223.0 0.7 fusion.12
  223.7 9.8 %custom-call.13 = f32[1,128,128]{1,2,0:T(8,128)S(1)} custom-call(f32[1,128,128]{2,1,0:T(8,128)S(1)} %fusion.12), custom_call_target="InvertDiagBlocksLowerTriangular" | custom-call | tf_op jit(solution)/shard_map/triangular_solve | solution.py:11
  233.5 0.6 convolution_subtract_fusion.2
  234.1 10.1 %fusion.77 = f32[2048,128]{1,0:T(8,128)} fusion(f32[2048,1024]{1,0:T(8,128)} %fusion.1, f32[1024,128]{1,0:T(8,128)S(1)} %convolution_subtract_fusion.2), kind=kOutput, calls=%fused_computation.122 | convolution fusion | flops 3221225472 | bytes 9961472 | tf_op jit(solution)/shard_map/dot_general | solution.py:76
  244.2 0.0 all-reduce.10.cloned.1.call-update
  244.2 0.0 all-reduce.12.cloned.1.call-start
  244.2 1.0 convolution_subtract_fusion.1
  245.2 16.6 %fusion.74 = f32[1024,128]{1,0:T(8,128)} fusion(f32[2048,1024]{1,0:T(8,128)} %fusion.1, f32[2048,128]{1,0:T(8,128)S(1)} %convolution_subtract_fusion.1), kind=kOutput, calls=%fused_computation.119 | convolution fusion | flops 3221225472 | bytes 9961472 | tf_op jit(solution)/shard_map/dot_general | solution.py:78
  261.8 41.8 %all-reduce.10.cloned.1.call-done = f32[2048,128]{1,0:T(8,128)} async-done(((f32[2048,128]{1,0:T(8,128)}), f32[2048,128]{1,0:T(8,128)}) %all-reduce.10.cloned.1.call-update) | async-done | bytes 1048592 | tf_op jit(solution)/shard_map/psum | solution.py:77
  303.7 3.7 fusion.79
  307.3 0.0 all-reduce.12.cloned.1.call-update
  307.3 46.2 %all-reduce.12.cloned.1.call-done = (f32[128,128]{1,0:T(8,128)}, f32[1024,128]{1,0:T(8,128)}, f32[128,128]{1,0:T(8,128)}) async-done(((f32[128,128]{1,0:T(8,128)}, f32[1024,128]{1,0:T(8,128)}, f32[128,128]{1,0:T(8,128)}), (f32[128,128]{1,0:T(8,128)}, f32[1024,128]{1,0:T(8,128)}, f32[128,128]{1,0:T(8,128)})) %all-reduce.12.cloned.1.call-update) | async-done | bytes 655376 | tf_op jit(solution)/shard_map/psum | solution.py:54
  353.6 1.1 fusion.25
  354.7 0.3 fusion.24
  355.0 0.1 copy.17
  355.1 11.7 %cholesky.55 = f32[128,128]{1,0:T(8,128)S(1)} custom-call(f32[128,128]{1,0:T(8,128)S(1)} %fusion.23), custom_call_target="Cholesky" | custom-call | tf_op jit(solution)/shard_map/jit(cholesky)/cholesky | solution.py:16
  366.8 0.6 compare_reduce_fusion
  367.4 0.6 fusion.13
  368.0 9.8 %custom-call.14 = f32[1,128,128]{1,2,0:T(8,128)S(1)} custom-call(f32[1,128,128]{2,1,0:T(8,128)S(1)} %fusion.13), custom_call_target="InvertDiagBlocksLowerTriangular" | custom-call | tf_op jit(solution)/shard_map/triangular_solve | solution.py:18
  377.8 0.3 fusion.19
  378.1 0.2 fusion.21
  378.3 1.0 fusion.80
  379.4 0.3 fusion.81
  379.6 0.0 copy-start
  379.6 0.0 slice-start
  379.7 1.8 fusion.75
  381.4 0.0 slice-start.1
  381.4 7.2 %fusion.76 = f32[2048,1024]{1,0:T(8,128)S(1)} fusion(f32[2048,128]{1,0:T(8,128)S(1)} %convolution_subtract_fusion.1, f32[128,1024]{1,0:T(8,128)S(1)} %fusion.75), kind=kOutput, calls=%fused_computation.121 | convolution fusion | flops 3221225472 | bytes 9961472 | tf_op jit(solution)/shard_map/dot_general | solution.py:82
  388.7 0.0 copy-done
  388.7 1.0 fusion.78
  389.7 1.0 convolution_subtract_fusion
  390.7 0.0 slice-done
  390.7 0.0 slice-done.1
  390.7 8.0 %subtract_bitcast_fusion = f32[1,2048,1,1024]{3,1,2,0:T(8,128)S(1)} fusion(f32[2048,1024]{1,0:T(8,128)S(1)} %bitcast.83, f32[2048,1024]{1,0:T(8,128)S(1)} %fusion.76, f32[2048,128]{1,0:T(8,128)S(1)} %convolution_subtract_fusion, f32[1024,128]{1,0:T(8,128)S(1)} %convolution_subtract_fusion.2), kind=kOutput, calls=%fused_computation.4 | convolution fusion | flops 3225419776 | bytes 26738688 | tf_op jit(solution)/shard_map/dot_general | solution.py:83
  398.7 16.1 %copy.18 = f32[1,2048,1,1024]{3,2,1,0:T(1,128)} copy(f32[1,2048,1,1024]{3,1,2,0:T(8,128)S(1)} %subtract_bitcast_fusion) | data formatting | bytes 16777216 | tf_op jit(solution)/shard_map/broadcast_in_dim | solution.py:88
  (11 shorter events, 0.2 us)
Async XLA Ops:
  6.5 151.3 %all-reduce.6.cloned.1.call-start = ((), (), s32[]{:S(2)}) async-start(), calls=%async_computation | async-start | bytes 8388608 | tf_op jit(solution)/shard_map/psum | solution.py:41
  12.3 196.4 %all-reduce.8.cloned.1.call-start = ((), (), s32[]{:S(2)}) async-start(), calls=%async_computation.1 | async-start | bytes 131072 | tf_op jit(solution)/shard_map/psum | solution.py:54
  167.5 136.2 %all-reduce.10.cloned.1.call-start = ((), (), s32[]{:S(2)}) async-start(), calls=%async_computation.2 | async-start | bytes 2097152 | tf_op jit(solution)/shard_map/psum | solution.py:77
  244.2 109.4 %all-reduce.12.cloned.1.call-start = ((), (), s32[]{:S(2)}) async-start(), calls=%async_computation.3 | async-start | bytes 1310720 | tf_op jit(solution)/shard_map/psum | solution.py:54
  379.6 9.0 %copy-start = (f32[2048,128]{1,0:T(8,128)S(1)}, f32[2048,128]{1,0:T(8,128)}, u32[]{:S(2)}) copy-start(f32[2048,128]{1,0:T(8,128)} %all-reduce.10.cloned.1.call-done) | copy-start | bytes 3145732
  379.6 11.0 %slice-start = ((s8[8388608]{0:T(1024)(128)(4,1)}), s8[4194304]{0:T(1024)(128)(4,1)S(1)}, s32[]{:S(2)}) async-start(s8[8388608]{0:T(1024)(128)(4,1)} %bitcast.82), calls=%async_computation.4 | async-start | bytes 8388608
  381.4 9.3 %slice-start.1 = ((s8[8388608]{0:T(1024)(128)(4,1)}), s8[4194304]{0:T(1024)(128)(4,1)S(1)}, s32[]{:S(2)}) async-start(s8[8388608]{0:T(1024)(128)(4,1)} %bitcast.82), calls=%async_computation.5 | async-start | bytes 8388608
Sparse Core Ops, SparseCore 0:
  12.9 144.9 all-reduce.5
  167.6 41.1 all-reduce.7
  244.3 59.2 all-reduce.9
  307.5 46.0 all-reduce.11
where the time goes:
time: 428 us; the launch traced here: 422 us
  waiting for transfers between devices  257 us (60%)
  matrix products  77.7 us (18%)
  other arithmetic  49.6 us (12%)
  local copies, waits for them, and re-layouts  22.7 us (5%)
  between operations  14.3 us (3%)
    psum x1, waiting for transfers between devices, per_device(): whole = lax.psum(partial_value, ('row', 'col'))  145 us
    psum x2, waiting for transfers between devices, per_device(): gram, top_rows = lax.psum((gram_part, top_part), 'row')  70 us
    psum x1, waiting for transfers between devices, per_device(): zrows = lax.psum(zpart, 'col')  41.8 us
    dot_general x1, matrix products, per_device(): lax.dot_general(refreshed, reflect_r, (((0,), (0,)), ((), ())), precision...  16.6 us
    broadcast_in_dim x1, local copies, waits for them, and re-layouts, per_device(): return (refreshed - first - second)[None, :, None, :]  16.1 us
    another operation x3, other arithmetic, per_device(): factor = jnp.linalg.cholesky(gram)  12.5 us
    another operation x3, other arithmetic, invert_shifted(): factor = jnp.linalg.cholesky(normal)  12.4 us
    dot_general x1, matrix products, per_device(): lax.dot_general(row_select, scols, (((0,), (1,)), ((), ())), precision=HIGH)  11 us
  transfers between devices with their start and end apart: 4, of which 4 were waited for; matrix products, arithmetic and copies ran while one was open for 8% of the time, Pallas kernels for 0%

commit v1 on v0

--- a/solution.py
+++ b/solution.py
@@ -38,7 +38,7 @@
     partial_value = lax.dot_general(
         psi, hcols, (((0,), (0,)), ((), ())), preferred_element_type=jnp.float32
     )
-    whole = lax.psum(partial_value, ("row", "col"))
+    whole = lax.psum(lax.psum(partial_value, "row"), "col")
     prow = lax.dynamic_index_in_dim(
         whole.reshape(tiles_r, n_row, TILE, panel), prow_id, 1, keepdims=False
     ).reshape(local_rows, panel)

time: 428 us -> 488 us (1.14)
  waiting for transfers between devices: 257 us -> 318 us
    psum x1 -> x2, waiting for transfers between devices: 145 us -> 205 us  [per_device(): whole = lax.psum(lax.psum(partial_value, 'row'), 'col')]
  transfers between devices with their start and end apart: 4 -> 5, of which waited for: 4 -> 5; matrix products, arithmetic and copies ran while one was open for 8% -> 7% of each run, Pallas kernels for 0% -> 0%
where the time goes in v1:
time: 488 us; the launch traced here: 482 us
  waiting for transfers between devices  318 us (65%)
  matrix products  77.7 us (16%)
  other arithmetic  49.6 us (10%)
  local copies, waits for them, and re-layouts  22.7 us (5%)
  between operations  14.3 us (3%)
    psum x2, waiting for transfers between devices, per_device(): whole = lax.psum(lax.psum(partial_value, 'row'), 'col')  205 us
    psum x2, waiting for transfers between devices, per_device(): gram, top_rows = lax.psum((gram_part, top_part), 'row')  70.8 us
    psum x1, waiting for transfers between devices, per_device(): zrows = lax.psum(zpart, 'col')  41.8 us
    dot_general x1, matrix products, per_device(): lax.dot_general(refreshed, reflect_r, (((0,), (0,)), ((), ())), precision...  16.6 us
    broadcast_in_dim x1, local copies, waits for them, and re-layouts, per_device(): return (refreshed - first - second)[None, :, None, :]  16.1 us
    another operation x3, other arithmetic, per_device(): factor = jnp.linalg.cholesky(gram)  12.5 us
    another operation x3, other arithmetic, invert_shifted(): factor = jnp.linalg.cholesky(normal)  12.4 us
    dot_general x1, matrix products, per_device(): lax.dot_general(row_select, scols, (((0,), (1,)), ((), ())), precision=HIGH)  11 us
  transfers between devices with their start and end apart: 5, of which 5 were waited for; matrix products, arithmetic and copies ran while one was open for 7% of the time, Pallas kernels for 0%

profile of v1, /device:TPU:0, one launch (start us, length us, event | category | flops | bytes accessed | tf_op | source)
XLA Modules:
  0.0 482.1 jit_solution(243958844398236610)
XLA Ops:
  6.5 0.0 all-reduce.7.cloned.1.call-start
  7.2 5.1 %convolution_bitcast_fusion = f32[8192,128]{0,1:T(8,128)} fusion(bf16[256,8192]{1,0:T(8,128)(2,1)} %param.7, bf16[256,128]{1,0:T(8,128)(2,1)} %param.8, pred[256]{0:T(512)(128)(4,1)S(1)} %iota_compare_fusion.9), kind=kOutput, calls=%fused_computation | convolution fusion | flops 536903680 | bytes 8454400 | tf_op jit(solution)/shard_map/dot_general | solution.py:38
  12.3 0.0 all-reduce.7.cloned.1.call-update
  12.3 0.0 all-reduce.9.cloned.1.call-start
  12.4 106.4 %all-reduce.7.cloned.1.call-done = f32[8192,128]{0,1:T(8,128)} async-done(((f32[8192,128]{0,1:T(8,128)}), f32[8192,128]{0,1:T(8,128)}) %all-reduce.7.cloned.1.call-update) | async-done | bytes 4194320 | tf_op jit(solution)/shard_map/psum | solution.py:41
  118.8 0.0 all-reduce.9.cloned.1.call-update
  118.8 0.0 all-reduce.11.cloned.1.call-start
  119.0 0.1 fusion.18
  119.1 98.6 %all-reduce.9.cloned.1.call-done = f32[8192,128]{0,1:T(8,128)} async-done(((f32[8192,128]{0,1:T(8,128)}), f32[8192,128]{0,1:T(8,128)}) %all-reduce.9.cloned.1.call-update) | async-done | bytes 4194320 | tf_op jit(solution)/shard_map/psum | solution.py:41
  217.7 5.6 %copy.11 = f32[8192,128]{1,0:T(8,128)} copy(f32[8192,128]{0,1:T(8,128)} %all-reduce.9.cloned.1.call-done) | data formatting | bytes 8388608 | tf_op jit(solution)/shard_map/psum | solution.py:41
  223.2 1.6 broadcast_select_fusion
  224.8 2.4 convolution_bitcast_fusion.1
  227.3 0.0 all-reduce.11.cloned.1.call-update
  227.3 0.0 all-reduce.13.cloned.1.call-start
  227.3 3.6 fusion.10
  230.9 1.3 broadcast_select_fusion.1
  232.2 11.0 %fusion.1 = f32[2048,1024]{1,0:T(8,128)} fusion(f32[2048,1024]{1,0:T(8,128)S(1)} %fusion.10, f32[1,2048,1,1024]{3,2,1,0:T(1,128)} %param.10, pred[1024]{0:T(1024)(128)(4,1)S(1)} %broadcast_compare_fusion.1, pred[2048]{0:T(1024)(128)(4,1)S(1)} %broadcast_compare_fusion, f32[1024,128]{1,0:T(8,128)S(1)} %bitcast.89, s32[2048]{0:T(1024)S(1)} %fusion.60), kind=kOutput, calls=%fused_computation.3 | convolution fusion | flops 3234332672 | bytes 25701376 | tf_op jit(solution)/shard_map/dot_general | solution.py:68
  243.2 1.6 fusion.4
  244.8 24.5 %all-reduce.11.cloned.1.call-done = f32[128,128]{0,1:T(8,128)} async-done(((f32[128,128]{0,1:T(8,128)}), f32[128,128]{0,1:T(8,128)}) %all-reduce.11.cloned.1.call-update) | async-done | bytes 65552 | tf_op jit(solution)/shard_map/psum | solution.py:54
  269.3 0.9 copy.16
  270.3 0.9 fusion.29
  271.1 11.7 %cholesky.44 = f32[128,128]{1,0:T(8,128)S(1)} custom-call(f32[128,128]{1,0:T(8,128)S(1)} %fusion.29), custom_call_target="Cholesky" | custom-call | tf_op jit(solution)/shard_map/jit(cholesky)/cholesky | solution.py:55
  282.9 0.7 compare_reduce_fusion.1
  283.6 0.7 fusion.12
  284.3 9.8 %custom-call.13 = f32[1,128,128]{1,2,0:T(8,128)S(1)} custom-call(f32[1,128,128]{2,1,0:T(8,128)S(1)} %fusion.12), custom_call_target="InvertDiagBlocksLowerTriangular" | custom-call | tf_op jit(solution)/shard_map/triangular_solve | solution.py:11
  294.1 0.6 convolution_subtract_fusion.2
  294.7 10.1 %fusion.77 = f32[2048,128]{1,0:T(8,128)} fusion(f32[2048,1024]{1,0:T(8,128)} %fusion.1, f32[1024,128]{1,0:T(8,128)S(1)} %convolution_subtract_fusion.2), kind=kOutput, calls=%fused_computation.122 | convolution fusion | flops 3221225472 | bytes 9961472 | tf_op jit(solution)/shard_map/dot_general | solution.py:76
  304.7 0.0 all-reduce.13.cloned.1.call-update
  304.8 0.0 all-reduce.15.cloned.1.call-start
  304.8 1.0 convolution_subtract_fusion.1
  305.8 16.6 %fusion.74 = f32[1024,128]{1,0:T(8,128)} fusion(f32[2048,1024]{1,0:T(8,128)} %fusion.1, f32[2048,128]{1,0:T(8,128)S(1)} %convolution_subtract_fusion.1), kind=kOutput, calls=%fused_computation.119 | convolution fusion | flops 3221225472 | bytes 9961472 | tf_op jit(solution)/shard_map/dot_general | solution.py:78
  322.4 41.8 %all-reduce.13.cloned.1.call-done = f32[2048,128]{1,0:T(8,128)} async-done(((f32[2048,128]{1,0:T(8,128)}), f32[2048,128]{1,0:T(8,128)}) %all-reduce.13.cloned.1.call-update) | async-done | bytes 1048592 | tf_op jit(solution)/shard_map/psum | solution.py:77
  364.2 3.7 fusion.79
  367.9 0.0 all-reduce.15.cloned.1.call-update
  367.9 46.2 %all-reduce.15.cloned.1.call-done = (f32[128,128]{1,0:T(8,128)}, f32[1024,128]{1,0:T(8,128)}, f32[128,128]{1,0:T(8,128)}) async-done(((f32[128,128]{1,0:T(8,128)}, f32[1024,128]{1,0:T(8,128)}, f32[128,128]{1,0:T(8,128)}), (f32[128,128]{1,0:T(8,128)}, f32[1024,128]{1,0:T(8,128)}, f32[128,128]{1,0:T(8,128)})) %all-reduce.15.cloned.1.call-update) | async-done | bytes 655376 | tf_op jit(solution)/shard_map/psum | solution.py:54
  414.1 1.1 fusion.25
  415.3 0.3 fusion.24
  415.5 0.1 copy.17
  415.7 11.7 %cholesky.55 = f32[128,128]{1,0:T(8,128)S(1)} custom-call(f32[128,128]{1,0:T(8,128)S(1)} %fusion.23), custom_call_target="Cholesky" | custom-call | tf_op jit(solution)/shard_map/jit(cholesky)/cholesky | solution.py:16
  427.4 0.6 compare_reduce_fusion
  428.0 0.6 fusion.13
  428.6 9.8 %custom-call.14 = f32[1,128,128]{1,2,0:T(8,128)S(1)} custom-call(f32[1,128,128]{2,1,0:T(8,128)S(1)} %fusion.13), custom_call_target="InvertDiagBlocksLowerTriangular" | custom-call | tf_op jit(solution)/shard_map/triangular_solve | solution.py:18
  438.4 0.3 fusion.19
  438.7 0.2 fusion.21
  438.9 1.0 fusion.80
  440.0 0.3 fusion.81
  440.2 0.0 copy-start
  440.2 0.0 slice-start
  440.2 1.8 fusion.75
  442.0 0.0 slice-start.1
  442.0 7.2 %fusion.76 = f32[2048,1024]{1,0:T(8,128)S(1)} fusion(f32[2048,128]{1,0:T(8,128)S(1)} %convolution_subtract_fusion.1, f32[128,1024]{1,0:T(8,128)S(1)} %fusion.75), kind=kOutput, calls=%fused_computation.121 | convolution fusion | flops 3221225472 | bytes 9961472 | tf_op jit(solution)/shard_map/dot_general | solution.py:82
  449.2 0.0 copy-done
  449.3 1.0 fusion.78
  450.3 1.0 convolution_subtract_fusion
  451.3 0.0 slice-done
  451.3 0.0 slice-done.1
  451.3 8.0 %subtract_bitcast_fusion = f32[1,2048,1,1024]{3,1,2,0:T(8,128)S(1)} fusion(f32[2048,1024]{1,0:T(8,128)S(1)} %bitcast.83, f32[2048,1024]{1,0:T(8,128)S(1)} %fusion.76, f32[2048,128]{1,0:T(8,128)S(1)} %convolution_subtract_fusion, f32[1024,128]{1,0:T(8,128)S(1)} %convolution_subtract_fusion.2), kind=kOutput, calls=%fused_computation.4 | convolution fusion | flops 3225419776 | bytes 26738688 | tf_op jit(solution)/shard_map/dot_general | solution.py:83
  459.3 16.1 %copy.18 = f32[1,2048,1,1024]{3,2,1,0:T(1,128)} copy(f32[1,2048,1,1024]{3,1,2,0:T(8,128)S(1)} %subtract_bitcast_fusion) | data formatting | bytes 16777216 | tf_op jit(solution)/shard_map/broadcast_in_dim | solution.py:88
  (11 shorter events, 0.2 us)
Async XLA Ops:
  6.5 112.3 %all-reduce.7.cloned.1.call-start = ((), (), s32[]{:S(2)}) async-start(), calls=%async_computation | async-start | bytes 8388608 | tf_op jit(solution)/shard_map/psum | solution.py:41
  12.3 205.4 %all-reduce.9.cloned.1.call-start = ((), (), s32[]{:S(2)}) async-start(), calls=%async_computation.1 | async-start | bytes 8388608 | tf_op jit(solution)/shard_map/psum | solution.py:41
  118.8 150.5 %all-reduce.11.cloned.1.call-start = ((), (), s32[]{:S(2)}) async-start(), calls=%async_computation.2 | async-start | bytes 131072 | tf_op jit(solution)/shard_map/psum | solution.py:54
  227.3 136.9 %all-reduce.13.cloned.1.call-start = ((), (), s32[]{:S(2)}) async-start(), calls=%async_computation.3 | async-start | bytes 2097152 | tf_op jit(solution)/shard_map/psum | solution.py:77
  304.8 109.4 %all-reduce.15.cloned.1.call-start = ((), (), s32[]{:S(2)}) async-start(), calls=%async_computation.4 | async-start | bytes 1310720 | tf_op jit(solution)/shard_map/psum | solution.py:54
  440.2 9.0 %copy-start = (f32[2048,128]{1,0:T(8,128)S(1)}, f32[2048,128]{1,0:T(8,128)}, u32[]{:S(2)}) copy-start(f32[2048,128]{1,0:T(8,128)} %all-reduce.13.cloned.1.call-done) | copy-start | bytes 3145732
  440.2 11.0 %slice-start = ((s8[8388608]{0:T(1024)(128)(4,1)}), s8[4194304]{0:T(1024)(128)(4,1)S(1)}, s32[]{:S(2)}) async-start(s8[8388608]{0:T(1024)(128)(4,1)} %bitcast.82), calls=%async_computation.5 | async-start | bytes 8388608
  442.0 9.3 %slice-start.1 = ((s8[8388608]{0:T(1024)(128)(4,1)}), s8[4194304]{0:T(1024)(128)(4,1)S(1)}, s32[]{:S(2)}) async-start(s8[8388608]{0:T(1024)(128)(4,1)} %bitcast.82), calls=%async_computation.6 | async-start | bytes 8388608
Sparse Core Ops, SparseCore 0:
  12.4 106.3 all-reduce.6
  121.2 96.4 all-reduce.8
  227.4 41.8 all-reduce.10
  304.9 59.2 all-reduce.12
  368.0 46.0 all-reduce.14
